TPU v7x, 32 devices: a whole 2x2x4 slice. The times are simulated.
32 devices in a mesh: seq: 4 (over y, x), wshard: 8 (over z, core).
Axes of the slice: x: 2, y: 2, z: 4, core: 2. Of those that a mesh axis runs over, the one named last changes fastest.
Arguments:
- layer_input: bfloat16 [8, 1024, 1536], P('wshard', 'seq'), may hold values from -6 to 6
- lengths: int32 [8], P('wshard'), may hold values from 256 to 1024, as said below
- norm_attn: float32 [1536], replicated, may hold values from 0.1 to 1.9
- w_query: bfloat16 [1536, 1536], P('wshard'), may hold values from -0.15625 to 0.15625
- w_key: bfloat16 [1536, 1536], P('wshard'), may hold values from -0.15625 to 0.15625
- w_value: bfloat16 [1536, 1536], P('wshard'), may hold values from -0.15625 to 0.15625
- w_ogate: bfloat16 [1536, 1536], P('wshard'), may hold values from -0.15625 to 0.15625
- w_forget: bfloat16 [1536, 24], P('wshard'), may hold values from -0.15625 to 0.15625
- forget_bias: float32 [24], replicated, may hold values from 3.5 to 8
- w_out: bfloat16 [1536, 1536], P('wshard'), may hold values from -1 to 1
- norm_ffn: float32 [1536], replicated, may hold values from 0.1 to 1.9
- w_gate: bfloat16 [1536, 4096], P('wshard'), may hold values from -0.15625 to 0.15625
- w_up: bfloat16 [1536, 4096], P('wshard'), may hold values from -0.15625 to 0.15625
- w_down: bfloat16 [4096, 1536], P('wshard'), may hold values from -0.09375 to 0.09375
- output_grad: bfloat16 [8, 1024, 1536], P('wshard', 'seq'), may hold values from -6 to 6
Outputs:
- layer_output: bfloat16 [8, 1024, 1536], P('wshard', 'seq')
- grad_input: float32 [8, 1024, 1536], P('wshard', 'seq')
- grad_norm_attn: float32 [1536], replicated
- grad_w_query: float32 [1536, 1536], P('wshard')
- grad_w_key: float32 [1536, 1536], P('wshard')
- grad_w_value: float32 [1536, 1536], P('wshard')
- grad_w_ogate: float32 [1536, 1536], P('wshard')
- grad_w_forget: float32 [1536, 24], P('wshard')
- grad_forget_bias: float32 [24], replicated
- grad_w_out: float32 [1536, 1536], P('wshard')
- grad_norm_ffn: float32 [1536], replicated
- grad_w_gate: float32 [1536, 4096], P('wshard')
- grad_w_up: float32 [1536, 4096], P('wshard')
- grad_w_down: float32 [4096, 1536], P('wshard')
Inputs may be any that keep to these rules, and one draw needn't show every extreme that they name: Each sequence has 1024 slots of which the first lengths[s] are valid; in every draw one sequence is full and one has exactly 256 valid slots.
All inputs are finite; a program needn't handle non-finite values.
Results may differ from a plain program's by a relative error of at most 0.014.
Values may be sent and summed in bfloat16 or wider, within the bound.
A program may use at most 320 MiB of HBM per device.

v0:
```python
import jax
import jax.numpy as jnp
from jax import lax
from jax.sharding import PartitionSpec as P

EPS = 1e-06
NEG_FILL = -1e30


def product(left, right):
    return jnp.dot(left, right, preferred_element_type=jnp.float32)


def product_tn(left, right):
    return lax.dot_general(
        left, right, (((0,), (0,)), ((), ())), preferred_element_type=jnp.float32
    )


def product_nt(left, right):
    return lax.dot_general(
        left, right, (((1,), (1,)), ((), ())), preferred_element_type=jnp.float32
    )


def rms_norm(values, gain):
    return values * lax.rsqrt(jnp.mean(values * values, axis=-1, keepdims=True) + EPS) * gain


def gate_product(attended, gate_pre):
    return attended * jax.nn.sigmoid(gate_pre)


def swiglu(gate, upward):
    return jax.nn.silu(gate) * upward


def block_scores(query_block, key_block, cum_rows, cum_keys, first_row, length, scale):
    plain = (
        jnp.einsum("qhd,khd->hqk", query_block, key_block, preferred_element_type=jnp.float32)
        * scale
    )
    plain = plain + cum_rows.T[:, :, None] - cum_keys.T[:, None, :]
    rows = first_row + jnp.arange(query_block.shape[0], dtype=jnp.int32)
    columns = jnp.arange(key_block.shape[0], dtype=jnp.int32)
    allowed = (columns[None, :] <= rows[:, None]) & (columns[None, :] < length)
    return jnp.where(allowed[None], plain, NEG_FILL)


def on_device(
    layer_input,
    lengths,
    norm_attn,
    w_query,
    w_key,
    w_value,
    w_ogate,
    w_forget,
    forget_bias,
    w_out,
    norm_ffn,
    w_gate,
    w_up,
    w_down,
    output_grad,
):
    tokens = layer_input.shape[1]
    heads = forget_bias.shape[0]
    groups = lax.axis_size("seq")
    local_heads = heads // groups
    head_size = layer_input.shape[2] // heads
    slots = tokens * groups
    block = min(512, slots)
    scale = head_size ** (-0.5)
    length = lengths[0]
    seq_rank = lax.axis_index("seq")
    positions = seq_rank * tokens + jnp.arange(tokens, dtype=jnp.int32)
    valid_slots = (positions < length).astype(jnp.float32)[:, None]
    inputs = layer_input[0].astype(jnp.float32)
    cotangent = output_grad[0].astype(jnp.float32) * valid_slots
    full_query, full_key, full_value, full_ogate, full_forget, full_out = (
        lax.all_gather(w_query, "wshard", axis=0, tiled=True),
        lax.all_gather(w_key, "wshard", axis=0, tiled=True),
        lax.all_gather(w_value, "wshard", axis=0, tiled=True),
        lax.all_gather(w_ogate, "wshard", axis=0, tiled=True),
        lax.all_gather(w_forget, "wshard", axis=0, tiled=True),
        lax.all_gather(w_out, "wshard", axis=0, tiled=True),
    )
    normed_attn = rms_norm(inputs, norm_attn).astype(jnp.bfloat16)
    queries = product(normed_attn, full_query).astype(jnp.bfloat16)
    keys_proj = product(normed_attn, full_key).astype(jnp.bfloat16)
    values_proj = product(normed_attn, full_value).astype(jnp.bfloat16)
    gate_pre = product(normed_attn, full_ogate)
    forget_pre = product(normed_attn, full_forget).astype(jnp.bfloat16)
    head_query, head_key, head_value, head_forget = (
        lax.all_to_all(queries, "seq", split_axis=1, concat_axis=0, tiled=True),
        lax.all_to_all(keys_proj, "seq", split_axis=1, concat_axis=0, tiled=True),
        lax.all_to_all(values_proj, "seq", split_axis=1, concat_axis=0, tiled=True),
        lax.all_to_all(forget_pre, "seq", split_axis=1, concat_axis=0, tiled=True),
    )
    head_query = head_query.reshape(slots, local_heads, head_size)
    head_key = head_key.reshape(slots, local_heads, head_size)
    head_value = head_value.reshape(slots, local_heads, head_size)
    bias_local = lax.dynamic_slice_in_dim(forget_bias, seq_rank * local_heads, local_heads)
    forget_total = head_forget.astype(jnp.float32) + bias_local
    log_forget, pull_forget = jax.vjp(jax.nn.log_sigmoid, forget_total)
    cumulative = jnp.cumsum(log_forget, axis=0)
    attn_blocks = []
    log_totals = []
    for number in range(slots // block):
        first = number * block
        last = first + block
        masked = block_scores(
            head_query[first:last],
            head_key[:last],
            cumulative[first:last],
            cumulative[:last],
            first,
            length,
            scale,
        )
        log_total = jax.nn.logsumexp(masked, axis=-1, keepdims=True)
        probability = jnp.exp(masked - log_total).astype(jnp.bfloat16)
        attn_blocks.append(
            jnp.einsum(
                "hqk,khd->qhd", probability, head_value[:last], preferred_element_type=jnp.float32
            )
        )
        log_totals.append(log_total)
    head_output = (
        jnp.concatenate(attn_blocks, axis=0)
        .reshape(slots, local_heads * head_size)
        .astype(jnp.bfloat16)
    )
    attended = lax.all_to_all(head_output, "seq", split_axis=0, concat_axis=1, tiled=True).astype(
        jnp.float32
    )
    gated_full, pull_gate = jax.vjp(gate_product, attended, gate_pre)
    gated = gated_full.astype(jnp.bfloat16)
    middle = inputs + product(gated, full_out)
    full_gate, full_up, full_down = (
        lax.all_gather(w_gate, "wshard", axis=0, tiled=True),
        lax.all_gather(w_up, "wshard", axis=0, tiled=True),
        lax.all_gather(w_down, "wshard", axis=0, tiled=True),
    )
    normed_ffn_full, pull_ffn_norm = jax.vjp(rms_norm, middle, norm_ffn)
    normed_ffn = normed_ffn_full.astype(jnp.bfloat16)
    gate_value = product(normed_ffn, full_gate)
    up_value = product(normed_ffn, full_up)
    hidden_full, pull_swiglu = jax.vjp(swiglu, gate_value, up_value)
    hidden = hidden_full.astype(jnp.bfloat16)
    result = middle + product(hidden, full_down)
    layer_output = result.astype(jnp.bfloat16)[None]
    full_gate, full_up, full_down = (
        lax.all_gather(w_gate, "wshard", axis=0, tiled=True),
        lax.all_gather(w_up, "wshard", axis=0, tiled=True),
        lax.all_gather(w_down, "wshard", axis=0, tiled=True),
    )
    cotangent_low = cotangent.astype(jnp.bfloat16)
    grad_w_down = product_tn(hidden, cotangent_low)
    grad_hidden = product_nt(cotangent_low, full_down)
    grad_gate_full, grad_up_full = pull_swiglu(grad_hidden)
    grad_gate = grad_gate_full.astype(jnp.bfloat16)
    grad_up = grad_up_full.astype(jnp.bfloat16)
    grad_w_gate = product_tn(normed_ffn, grad_gate)
    grad_w_up = product_tn(normed_ffn, grad_up)
    share_gate, share_up, share_down = (
        lax.psum_scatter(grad_w_gate, "wshard", scatter_dimension=0, tiled=True),
        lax.psum_scatter(grad_w_up, "wshard", scatter_dimension=0, tiled=True),
        lax.psum_scatter(grad_w_down, "wshard", scatter_dimension=0, tiled=True),
    )
    grad_normed_ffn = product_nt(grad_gate, full_gate) + product_nt(grad_up, full_up)
    grad_middle_part, grad_norm_ffn = pull_ffn_norm(grad_normed_ffn)
    grad_middle = cotangent + grad_middle_part
    full_query, full_key, full_value, full_ogate, full_forget, full_out = (
        lax.all_gather(w_query, "wshard", axis=0, tiled=True),
        lax.all_gather(w_key, "wshard", axis=0, tiled=True),
        lax.all_gather(w_value, "wshard", axis=0, tiled=True),
        lax.all_gather(w_ogate, "wshard", axis=0, tiled=True),
        lax.all_gather(w_forget, "wshard", axis=0, tiled=True),
        lax.all_gather(w_out, "wshard", axis=0, tiled=True),
    )
    grad_branch = grad_middle.astype(jnp.bfloat16)
    grad_w_out = product_tn(gated, grad_branch)
    grad_gated = product_nt(grad_branch, full_out)
    grad_attended_full, grad_gate_pre_full = pull_gate(grad_gated)
    grad_attended = grad_attended_full.astype(jnp.bfloat16)
    grad_gate_pre = grad_gate_pre_full.astype(jnp.bfloat16)
    head_grad = lax.all_to_all(
        grad_attended, "seq", split_axis=1, concat_axis=0, tiled=True
    ).reshape(slots, local_heads, head_size)
    grad_query_blocks = []
    grad_keys = jnp.zeros((slots, local_heads, head_size), jnp.float32)
    grad_values = jnp.zeros((slots, local_heads, head_size), jnp.float32)
    grad_cum = jnp.zeros((slots, local_heads), jnp.float32)
    for number in range(slots // block):
        first = number * block
        last = first + block
        masked = block_scores(
            head_query[first:last],
            head_key[:last],
            cumulative[first:last],
            cumulative[:last],
            first,
            length,
            scale,
        )
        probability = jnp.exp(masked - log_totals[number])
        probability_low = probability.astype(jnp.bfloat16)
        grad_block = head_grad[first:last]
        grad_probability = jnp.einsum(
            "qhd,khd->hqk", grad_block, head_value[:last], preferred_element_type=jnp.float32
        )
        row_dot = jnp.sum(grad_probability * probability, axis=-1, keepdims=True)
        score_terms = probability * (grad_probability - row_dot)
        grad_scores = score_terms.astype(jnp.bfloat16)
        grad_cum = grad_cum.at[first:last].add(jnp.sum(score_terms, axis=2).T)
        grad_cum = grad_cum.at[:last].add(-jnp.sum(score_terms, axis=1).T)
        grad_query_blocks.append(
            jnp.einsum(
                "hqk,khd->qhd", grad_scores, head_key[:last], preferred_element_type=jnp.float32
            )
            * scale
        )
        grad_keys = grad_keys.at[:last].add(
            jnp.einsum(
                "hqk,qhd->khd",
                grad_scores,
                head_query[first:last],
                preferred_element_type=jnp.float32,
            )
            * scale
        )
        grad_values = grad_values.at[:last].add(
            jnp.einsum(
                "hqk,qhd->khd", probability_low, grad_block, preferred_element_type=jnp.float32
            )
        )
    grad_head_query = (
        jnp.concatenate(grad_query_blocks, axis=0)
        .reshape(slots, local_heads * head_size)
        .astype(jnp.bfloat16)
    )
    grad_head_key = grad_keys.reshape(slots, local_heads * head_size).astype(jnp.bfloat16)
    grad_head_value = grad_values.reshape(slots, local_heads * head_size).astype(jnp.bfloat16)
    grad_log_forget = jnp.flip(jnp.cumsum(jnp.flip(grad_cum, 0), axis=0), 0)
    grad_forget_total = pull_forget(grad_log_forget)[0]
    grad_bias_local = jnp.sum(grad_forget_total, axis=0)
    grad_head_forget = grad_forget_total.astype(jnp.bfloat16)
    grad_bias = lax.dynamic_update_slice_in_dim(
        jnp.zeros((heads,), jnp.float32), grad_bias_local, seq_rank * local_heads, 0
    )
    grad_query_tok, grad_key_tok, grad_value_tok, grad_forget_tok = (
        lax.all_to_all(grad_head_query, "seq", split_axis=0, concat_axis=1, tiled=True),
        lax.all_to_all(grad_head_key, "seq", split_axis=0, concat_axis=1, tiled=True),
        lax.all_to_all(grad_head_value, "seq", split_axis=0, concat_axis=1, tiled=True),
        lax.all_to_all(grad_head_forget, "seq", split_axis=0, concat_axis=1, tiled=True),
    )
    grad_w_query = product_tn(normed_attn, grad_query_tok)
    grad_w_key = product_tn(normed_attn, grad_key_tok)
    grad_w_value = product_tn(normed_attn, grad_value_tok)
    grad_w_ogate = product_tn(normed_attn, grad_gate_pre)
    grad_w_forget = product_tn(normed_attn, grad_forget_tok)
    grad_normed_attn = (
        product_nt(grad_query_tok, full_query)
        + product_nt(grad_key_tok, full_key)
        + product_nt(grad_value_tok, full_value)
        + product_nt(grad_gate_pre, full_ogate)
        + product_nt(grad_forget_tok, full_forget)
    )
    unused_normed, pull_attn_norm = jax.vjp(rms_norm, inputs, norm_attn)
    grad_input_part, grad_norm_attn = pull_attn_norm(grad_normed_attn)
    grad_input = (grad_middle + grad_input_part)[None]
    share_query, share_key, share_value, share_ogate, share_forget, share_out = (
        lax.psum_scatter(grad_w_query, "wshard", scatter_dimension=0, tiled=True),
        lax.psum_scatter(grad_w_key, "wshard", scatter_dimension=0, tiled=True),
        lax.psum_scatter(grad_w_value, "wshard", scatter_dimension=0, tiled=True),
        lax.psum_scatter(grad_w_ogate, "wshard", scatter_dimension=0, tiled=True),
        lax.psum_scatter(grad_w_forget, "wshard", scatter_dimension=0, tiled=True),
        lax.psum_scatter(grad_w_out, "wshard", scatter_dimension=0, tiled=True),
    )
    summed = lax.psum(
        (
            share_query,
            share_key,
            share_value,
            share_ogate,
            share_forget,
            share_out,
            share_gate,
            share_up,
            share_down,
        ),
        "seq",
    )
    small = lax.psum((grad_norm_attn, grad_norm_ffn, grad_bias), ("seq", "wshard"))
    return (
        layer_output,
        grad_input,
        small[0],
        summed[0],
        summed[1],
        summed[2],
        summed[3],
        summed[4],
        small[2],
        summed[5],
        small[1],
        summed[6],
        summed[7],
        summed[8],
    )


def solution(mesh):
    return jax.shard_map(
        on_device,
        mesh=mesh,
        in_specs=(
            P("wshard", "seq", None),
            P("wshard"),
            P(),
            P("wshard", None),
            P("wshard", None),
            P("wshard", None),
            P("wshard", None),
            P("wshard", None),
            P(),
            P("wshard", None),
            P(),
            P("wshard", None),
            P("wshard", None),
            P("wshard", None),
            P("wshard", "seq", None),
        ),
        out_specs=(
            P("wshard", "seq", None),
            P("wshard", "seq", None),
            P(),
            P("wshard", None),
            P("wshard", None),
            P("wshard", None),
            P("wshard", None),
            P("wshard", None),
            P(),
            P("wshard", None),
            P(),
            P("wshard", None),
            P("wshard", None),
            P("wshard", None),
        ),
        check_vma=False,
    )
```

profile of v0, /device:TPU:0, one launch (start us, length us, event | category | flops | bytes accessed | tf_op | source)
XLA Modules:
  0.0 2250.1 jit_solution(14034626148076068896)
XLA Ops:
  12.7 16.2 all-gather
  34.6 29.3 %all-gather.10.cloned.1.call-done = bf16[1536,1536]{1,0:T(8,128)(2,1)} async-done(((bf16[192,1536]{1,0:T(8,128)(2,1)}), bf16[1536,1536]{1,0:T(8,128)(2,1)}) %all-gather.10.cloned.1.call-update) | async-done | bytes 4718608 | tf_op jit(solution)/shard_map/all_gather | solution.py:84
  73.6 42.0 %all-gather.14.cloned.1.call-done = bf16[1536,1536]{1,0:T(8,128)(2,1)} async-done(((bf16[192,1536]{1,0:T(8,128)(2,1)}), bf16[1536,1536]{1,0:T(8,128)(2,1)}) %all-gather.14.cloned.1.call-update) | async-done | bytes 4718608 | tf_op jit(solution)/shard_map/all_gather | solution.py:83
  124.8 42.4 %all-gather.12.cloned.1.call-done = bf16[1536,1536]{1,0:T(8,128)(2,1)} async-done(((bf16[192,1536]{1,0:T(8,128)(2,1)}), bf16[1536,1536]{1,0:T(8,128)(2,1)}) %all-gather.12.cloned.1.call-update) | async-done | bytes 4718608 | tf_op jit(solution)/shard_map/all_gather | solution.py:82
  237.5 32.7 %all-gather.18.cloned.1.call-done = bf16[1536,1536]{1,0:T(8,128)(2,1)} async-done(((bf16[192,1536]{1,0:T(8,128)(2,1)}), bf16[1536,1536]{1,0:T(8,128)(2,1)}) %all-gather.18.cloned.1.call-update) | async-done | bytes 4718608 | tf_op jit(solution)/shard_map/all_gather | solution.py:87
  274.3 112.9 %all-gather.20.cloned.1.call-done = bf16[1536,4096]{1,0:T(8,128)(2,1)} async-done(((bf16[192,4096]{1,0:T(8,128)(2,1)}), bf16[1536,4096]{1,0:T(8,128)(2,1)}) %all-gather.20.cloned.1.call-update) | async-done | bytes 12582928 | tf_op jit(solution)/shard_map/all_gather | solution.py:142
  396.7 107.1 %all-gather.22.cloned.1.call-done = bf16[1536,4096]{1,0:T(8,128)(2,1)} async-done(((bf16[192,4096]{1,0:T(8,128)(2,1)}), bf16[1536,4096]{1,0:T(8,128)(2,1)}) %all-gather.22.cloned.1.call-update) | async-done | bytes 12582928 | tf_op jit(solution)/shard_map/all_gather | solution.py:143
  513.3 107.1 %all-gather.24.cloned.1.call-done = bf16[4096,1536]{1,0:T(8,128)(2,1)} async-done(((bf16[512,1536]{1,0:T(8,128)(2,1)}), bf16[4096,1536]{1,0:T(8,128)(2,1)}) %all-gather.24.cloned.1.call-update) | async-done | bytes 12582928 | tf_op jit(solution)/shard_map/all_gather | solution.py:144
  672.4 15.4 all_to_all.154
  727.7 13.0 all_to_all.155
  758.9 12.0 all_to_all.156
  808.7 12.0 fusion.126
  821.2 12.0 fusion.127
  834.3 12.2 fusion.87
  862.3 100.2 %reduce-scatter.12.cloned.1.call-done = f32[192,1536]{1,0:T(8,128)} async-done(((f32[1536,1536]{1,0:T(8,128)}), f32[192,1536]{1,0:T(8,128)}) %reduce-scatter.12.cloned.1.call-update) | async-done | bytes 1179664 | tf_op jit(solution)/shard_map/reduce_scatter | solution.py:275
  962.6 100.1 %reduce-scatter.14.cloned.1.call-done = f32[192,1536]{1,0:T(8,128)} async-done(((f32[1536,1536]{1,0:T(8,128)}), f32[192,1536]{1,0:T(8,128)}) %reduce-scatter.14.cloned.1.call-update) | async-done | bytes 1179664 | tf_op jit(solution)/shard_map/reduce_scatter | solution.py:276
  1062.6 100.2 %reduce-scatter.16.cloned.1.call-done = f32[192,1536]{1,0:T(8,128)} async-done(((f32[1536,1536]{1,0:T(8,128)}), f32[192,1536]{1,0:T(8,128)}) %reduce-scatter.16.cloned.1.call-update) | async-done | bytes 1179664 | tf_op jit(solution)/shard_map/reduce_scatter | solution.py:277
  1162.9 247.8 %reduce-scatter.22.cloned.1.call-done = f32[192,4096]{1,0:T(8,128)} async-done(((f32[1536,4096]{1,0:T(8,128)}), f32[192,4096]{1,0:T(8,128)}) %reduce-scatter.22.cloned.1.call-update) | async-done | bytes 3145744 | tf_op jit(solution)/shard_map/reduce_scatter | solution.py:168
  1410.7 247.8 %reduce-scatter.24.cloned.1.call-done = f32[192,4096]{1,0:T(8,128)} async-done(((f32[1536,4096]{1,0:T(8,128)}), f32[192,4096]{1,0:T(8,128)}) %reduce-scatter.24.cloned.1.call-update) | async-done | bytes 3145744 | tf_op jit(solution)/shard_map/reduce_scatter | solution.py:169
  1658.5 247.8 %reduce-scatter.26.cloned.1.call-done = f32[512,1536]{1,0:T(8,128)} async-done(((f32[4096,1536]{1,0:T(8,128)}), f32[512,1536]{1,0:T(8,128)}) %reduce-scatter.26.cloned.1.call-update) | async-done | bytes 3145744 | tf_op jit(solution)/shard_map/reduce_scatter | solution.py:170
  1916.3 23.0 %reduce-scatter.28.cloned.1.call-done = f32[192,24]{1,0:T(8,128)} async-done(((f32[1536,24]{1,0:T(8,128)}), f32[192,24]{1,0:T(8,128)}) %reduce-scatter.28.cloned.1.call-update) | async-done | bytes 18448
  1940.3 18.0 psum.89
  1971.1 38.5 %all-reduce.3 = (f32[1536]{0:T(1024)}, f32[24]{0:T(128)}, f32[1536]{0:T(1024)}) all-reduce(f32[1536]{0:T(1024)S(1)} %get-tuple-element.140, f32[24]{0:T(128)S(1)} %negate_dynamic-update-slice_fusion, f32[1536]{0:T(1024)S(1)} %copy-done.60), channel_id=1, replica_groups=mesh['seq'=4,'wshard'=8] {'seq','wshard'}, use_global_device_ids=true, to_apply=%region_19.20 | all-reduce | flops 3096 | bytes 24768 | tf_op jit(solution)/shard_map/psum | solution.py:296
  2012.7 215.3 %all-reduce.7.cloned.1.call-done = (f32[192,1536]{1,0:T(8,128)}, f32[192,1536]{1,0:T(8,128)}, f32[192,1536]{1,0:T(8,128)}, f32[192,1536]{1,0:T(8,128)}, f32[192,...) async-done(((f32[192,1536]{1,0:T(8,128)}, f32[192,1536]{1,0:T(8,128)}, f32[192,1536]{1,0:T(8,128)}, f32[192,1536]{1,0:T(8,128)}, ...) | async-done | bytes 15335440 | tf_op jit(solution)/shard_map/psum | solution.py:282
  (334 shorter events, 329.1 us)
Async XLA Ops:
  7.2 56.7 %all-gather.10.cloned.1.call-start = ((), (), s32[]{:S(2)}) async-start(), calls=%async_computation.19 | async-start | bytes 5308416 | tf_op jit(solution)/shard_map/all_gather | solution.py:84
  7.9 107.7 %all-gather.14.cloned.1.call-start = ((), (), s32[]{:S(2)}) async-start(), calls=%async_computation.21 | async-start | bytes 5308416 | tf_op jit(solution)/shard_map/all_gather | solution.py:83
  8.7 158.6 %all-gather.12.cloned.1.call-start = ((), (), s32[]{:S(2)}) async-start(), calls=%async_computation.20 | async-start | bytes 5308416 | tf_op jit(solution)/shard_map/all_gather | solution.py:82
  9.4 222.5 %all-gather.16.cloned.1.call-start = ((), (), s32[]{:S(2)}) async-start(), calls=%async_computation.22 | async-start | bytes 5308416 | tf_op jit(solution)/shard_map/all_gather | solution.py:85
  10.0 260.2 %all-gather.18.cloned.1.call-start = ((), (), s32[]{:S(2)}) async-start(), calls=%async_computation.23 | async-start | bytes 5308416 | tf_op jit(solution)/shard_map/all_gather | solution.py:87
  10.6 376.7 %all-gather.20.cloned.1.call-start = ((), (), s32[]{:S(2)}) async-start(), calls=%async_computation.24 | async-start | bytes 14155776 | tf_op jit(solution)/shard_map/all_gather | solution.py:142
  11.2 492.6 %all-gather.22.cloned.1.call-start = ((), (), s32[]{:S(2)}) async-start(), calls=%async_computation.25 | async-start | bytes 14155776 | tf_op jit(solution)/shard_map/all_gather | solution.py:143
  11.9 608.4 %all-gather.24.cloned.1.call-start = ((), (), s32[]{:S(2)}) async-start(), calls=%async_computation.26 | async-start | bytes 14155776 | tf_op jit(solution)/shard_map/all_gather | solution.py:144
  30.3 38.4 %all-to-all-start.3 = ((bf16[256,4,6]{0,2,1:T(8,128)(2,1)}), bf16[256,4,6]{0,2,1:T(8,128)(2,1)S(1)}, u32[]{:S(2)}, u32[]{:S(2)}) async-start(bf16[256,4,6]{0,2,1:T(8,128)(2,1)} %all_to_all.125), calls=%async_computation.3 | async-start | bytes 32768 | tf_op jit(solution)/shard_map/all_to_all | solution.py:99
  68.7 51.6 %all-to-all-start = ((bf16[256,4,384]{2,0,1:T(8,128)(2,1)}), bf16[256,4,384]{2,0,1:T(8,128)(2,1)S(1)}, u32[]{:S(2)}, u32[]{:S(2)}) async-start(bf16[256,4,384]{2,0,1:T(8,128)(2,1)} %bitcast.242), calls=%async_computation | async-start | bytes 1572864 | tf_op jit(solution)/shard_map/all_to_all | solution.py:98
  120.3 51.6 %all-to-all-start.2 = ((bf16[256,4,384]{2,0,1:T(8,128)(2,1)}), bf16[256,4,384]{2,0,1:T(8,128)(2,1)S(1)}, u32[]{:S(2)}, u32[]{:S(2)}) async-start(bf16[256,4,384]{2,0,1:T(8,128)(2,1)} %bitcast.240), calls=%async_computation.2 | async-start | bytes 1572864 | tf_op jit(solution)/shard_map/all_to_all | solution.py:97
  172.0 15.1 all-to-all-start.1
  216.1 14.0 all-to-all-start.4
  219.6 639.7 %reduce-scatter.18.cloned.1.call-start = ((), (), s32[]{:S(2)}) async-start(), calls=%async_computation.30 | async-start | bytes 10616832 | tf_op jit(solution)/shard_map/reduce_scatter | solution.py:278
  274.0 368.3 %copy-start.7 = (f32[256,1536]{1,0:T(8,128)}, f32[256,1536]{1,0:T(8,128)S(1)}, u32[]{:S(2)}) copy-start(f32[256,1536]{1,0:T(8,128)S(1)} %get-tuple-element.177) | copy-start | bytes 4718596
  664.5 197.9 %reduce-scatter.20.cloned.1.call-start = ((), (), s32[]{:S(2)}) async-start(), calls=%async_computation.31 | async-start | bytes 10616832 | tf_op jit(solution)/shard_map/reduce_scatter | solution.py:280
  671.1 291.5 %reduce-scatter.12.cloned.1.call-start = ((), (), s32[]{:S(2)}) async-start(), calls=%async_computation.27 | async-start | bytes 10616832 | tf_op jit(solution)/shard_map/reduce_scatter | solution.py:275
  746.7 316.0 %reduce-scatter.14.cloned.1.call-start = ((), (), s32[]{:S(2)}) async-start(), calls=%async_computation.28 | async-start | bytes 10616832 | tf_op jit(solution)/shard_map/reduce_scatter | solution.py:276
  776.9 386.0 %reduce-scatter.16.cloned.1.call-start = ((), (), s32[]{:S(2)}) async-start(), calls=%async_computation.29 | async-start | bytes 10616832 | tf_op jit(solution)/shard_map/reduce_scatter | solution.py:277
  808.7 602.0 %reduce-scatter.22.cloned.1.call-start = ((), (), s32[]{:S(2)}) async-start(), calls=%async_computation.32 | async-start | bytes 28311552 | tf_op jit(solution)/shard_map/reduce_scatter | solution.py:168
  820.7 837.7 %reduce-scatter.24.cloned.1.call-start = ((), (), s32[]{:S(2)}) async-start(), calls=%async_computation.33 | async-start | bytes 28311552 | tf_op jit(solution)/shard_map/reduce_scatter | solution.py:169
  833.2 1073.1 %reduce-scatter.26.cloned.1.call-start = ((), (), s32[]{:S(2)}) async-start(), calls=%async_computation.34 | async-start | bytes 28311552 | tf_op jit(solution)/shard_map/reduce_scatter | solution.py:170
  846.5 1092.8 %reduce-scatter.28.cloned.1.call-start = ((), (), s32[]{:S(2)}) async-start(), calls=%async_computation.35 | async-start | bytes 884736
  859.3 1368.7 %all-reduce.7.cloned.1.call-start = ((), (), s32[]{:S(2)}) async-start(), calls=%async_computation.36 | async-start | bytes 30670848 | tf_op jit(solution)/shard_map/psum | solution.py:282
  (72 other events, 713.2 us)
Sparse Core Ops, SparseCore 0:
  9.6 54.2 all-gather.9
  65.6 49.9 all-gather.13
  117.2 49.9 all-gather.11
  168.7 49.9 all-gather.15
  220.2 49.9 all-gather.17
  271.7 115.4 all-gather.19
  388.9 114.8 all-gather.21
  505.4 114.8 all-gather.23
  664.6 97.6 reduce-scatter.17
  764.4 97.8 reduce-scatter.19
  864.6 97.8 reduce-scatter.11
  964.7 97.8 reduce-scatter.13
  1064.9 97.8 reduce-scatter.15
  1165.1 245.5 reduce-scatter.21
  1412.9 245.5 reduce-scatter.23
  1660.7 245.5 reduce-scatter.25
  1909.0 30.3 reduce-scatter.27
  1943.9 284.0 all-reduce.6
where the time goes:
time: 2260 us; the launch traced here: 2250 us
  waiting for transfers between devices  1780 us (79%)
  matrix products  204 us (9%)
  blocking collectives  131 us (6%)
  local copies, waits for them, and re-layouts  71.3 us (3%)
  other arithmetic  30 us (1%)
    reduce_scatter x1, waiting for transfers between devices, on_device(): lax.psum_scatter(grad_w_down, 'wshard', scatter_dimension=0, tiled=True)  248 us
    reduce_scatter x1, waiting for transfers between devices, on_device(): lax.psum_scatter(grad_w_gate, 'wshard', scatter_dimension=0, tiled=True)  248 us
    reduce_scatter x1, waiting for transfers between devices, on_device(): lax.psum_scatter(grad_w_up, 'wshard', scatter_dimension=0, tiled=True)  248 us
    psum x1, waiting for transfers between devices, on_device(): lax.psum((share_query, share_key, share_value, share_ogate, share_forget,...  215 us
    all_gather x1, waiting for transfers between devices, on_device(): lax.all_gather(w_gate, 'wshard', axis=0, tiled=True)  113 us
    all_gather x1, waiting for transfers between devices, on_device(): lax.all_gather(w_up, 'wshard', axis=0, tiled=True)  107 us
    all_gather x1, waiting for transfers between devices, on_device(): lax.all_gather(w_down, 'wshard', axis=0, tiled=True)  107 us
    reduce_scatter x1, waiting for transfers between devices, on_device(): lax.psum_scatter(grad_w_query, 'wshard', scatter_dimension=0, tiled=True)  100 us
  transfers between devices with their start and end apart: 23, of which 18 were waited for; matrix products, arithmetic and copies ran while one was open for 11% of the time, Pallas kernels for 0%

commit v1 on v0

v1 whole, which is shorter than its diff:
```python
import jax
import jax.numpy as jnp
from jax import lax
from jax.sharding import PartitionSpec as P

EPS = 1e-06
NEG_FILL = -1e30
BF16 = jnp.bfloat16
F32 = jnp.float32


def product(left, right):
    return jnp.dot(left, right, preferred_element_type=F32)


def product_tn(left, right):
    return lax.dot_general(left, right, (((0,), (0,)), ((), ())), preferred_element_type=F32)


def product_nt(left, right):
    return lax.dot_general(left, right, (((1,), (1,)), ((), ())), preferred_element_type=F32)


def rms_norm(values, gain):
    return values * lax.rsqrt(jnp.mean(values * values, axis=-1, keepdims=True) + EPS) * gain


def gate_product(attended, gate_pre):
    return attended * jax.nn.sigmoid(gate_pre)


def swiglu(gate, upward):
    return jax.nn.silu(gate) * upward


def gather_rows(shard):
    return lax.all_gather(shard, "wshard", axis=0, tiled=True)


def scatter_rows(partial):
    return lax.psum_scatter(partial.astype(BF16), "wshard", scatter_dimension=0, tiled=True)


def gather_slots(shard):
    return lax.all_gather(shard, "seq", axis=0, tiled=True)


def scatter_slots(partial):
    return lax.psum_scatter(
        partial.astype(BF16), "seq", scatter_dimension=0, tiled=True
    ).astype(F32)


def share_columns(share):
    return lax.all_gather(share, "seq", axis=1, tiled=True).astype(F32)


def block_scores(query_block, key_block, cum_rows, cum_keys, first_row, length, scale):
    plain = (
        jnp.einsum("qhd,khd->hqk", query_block, key_block, preferred_element_type=F32) * scale
    )
    plain = plain + cum_rows.T[:, :, None] - cum_keys.T[:, None, :]
    rows = first_row + jnp.arange(query_block.shape[0], dtype=jnp.int32)
    columns = jnp.arange(key_block.shape[0], dtype=jnp.int32)
    allowed = (columns[None, :] <= rows[:, None]) & (columns[None, :] < length)
    return jnp.where(allowed[None], plain, NEG_FILL)


def attention_forward(query, key, value, cumulative, length, scale, block):
    slots = query.shape[0]
    blocks = []
    log_totals = []
    for first in range(0, slots, block):
        last = first + block
        masked = block_scores(
            query[first:last], key[:last], cumulative[first:last], cumulative[:last],
            first, length, scale,
        )
        log_total = jax.nn.logsumexp(masked, axis=-1, keepdims=True)
        probability = jnp.exp(masked - log_total).astype(BF16)
        blocks.append(
            jnp.einsum("hqk,khd->qhd", probability, value[:last], preferred_element_type=F32)
        )
        log_totals.append(log_total)
    return jnp.concatenate(blocks, axis=0).astype(BF16), log_totals


def attention_backward(query, key, value, grad, cumulative, log_totals, length, scale, block):
    slots, heads, size = query.shape
    grad_query = []
    grad_key = jnp.zeros((slots, heads, size), F32)
    grad_value = jnp.zeros((slots, heads, size), F32)
    grad_cum = jnp.zeros((slots, heads), F32)
    for number, first in enumerate(range(0, slots, block)):
        last = first + block
        masked = block_scores(
            query[first:last], key[:last], cumulative[first:last], cumulative[:last],
            first, length, scale,
        )
        probability = jnp.exp(masked - log_totals[number])
        probability_low = probability.astype(BF16)
        grad_block = grad[first:last]
        grad_probability = jnp.einsum(
            "qhd,khd->hqk", grad_block, value[:last], preferred_element_type=F32
        )
        row_dot = jnp.sum(grad_probability * probability, axis=-1, keepdims=True)
        score_terms = probability * (grad_probability - row_dot)
        grad_scores = score_terms.astype(BF16)
        grad_cum = grad_cum.at[first:last].add(jnp.sum(score_terms, axis=2).T)
        grad_cum = grad_cum.at[:last].add(-jnp.sum(score_terms, axis=1).T)
        grad_query.append(
            jnp.einsum("hqk,khd->qhd", grad_scores, key[:last], preferred_element_type=F32)
        )
        grad_key = grad_key.at[:last].add(
            jnp.einsum("hqk,qhd->khd", grad_scores, query[first:last], preferred_element_type=F32)
        )
        grad_value = grad_value.at[:last].add(
            jnp.einsum("hqk,qhd->khd", probability_low, grad_block, preferred_element_type=F32)
        )
    grad_query = (jnp.concatenate(grad_query, axis=0) * scale).astype(BF16)
    return grad_query, (grad_key * scale).astype(BF16), grad_value.astype(BF16), grad_cum


def on_device(
    layer_input, lengths, norm_attn, w_query, w_key, w_value, w_ogate, w_forget, forget_bias,
    w_out, norm_ffn, w_gate, w_up, w_down, output_grad,
):
    tokens, width = layer_input.shape[1:]
    heads = forget_bias.shape[0]
    groups = lax.axis_size("seq")
    owners = lax.axis_size("wshard")
    local_heads = heads // groups
    head_size = width // heads
    slots = tokens * groups
    part = width // groups
    units = w_gate.shape[1]
    own_units = units // owners
    piece = own_units // groups
    local_units = units // groups
    block = min(512, slots)
    scale = head_size ** (-0.5)
    length = lengths[0]
    rank = lax.axis_index("seq")
    positions = rank * tokens + jnp.arange(tokens, dtype=jnp.int32)
    valid_slots = (positions < length).astype(F32)[:, None]
    inputs = layer_input[0].astype(F32)
    cotangent = output_grad[0].astype(F32) * valid_slots

    def columns(weight):
        return lax.dynamic_slice_in_dim(weight, rank * part, part, 1)

    def unit_columns(weight):
        cut = lax.dynamic_index_in_dim(
            weight.reshape(-1, owners, groups, piece), rank, 2, keepdims=False
        )
        return cut.reshape(-1, local_units)

    pad = (-local_heads) % 128
    forget_columns = jnp.pad(
        lax.dynamic_slice_in_dim(w_forget, rank * local_heads, local_heads, 1), ((0, 0), (0, pad))
    )
    normed_attn = gather_slots(rms_norm(inputs, norm_attn).astype(BF16))
    full_attn = gather_rows(
        jnp.concatenate(
            [columns(w_query), columns(w_key), columns(w_value), columns(w_ogate), forget_columns],
            axis=1,
        )
    )
    cut_out = gather_rows(columns(w_out))
    full_out = lax.all_to_all(cut_out, "seq", split_axis=0, concat_axis=1, tiled=True)
    full_gate_up = gather_rows(
        jnp.concatenate([unit_columns(w_gate), unit_columns(w_up)], axis=1)
    )
    full_down = gather_rows(lax.dynamic_slice_in_dim(w_down, rank * piece, piece, 0))
    cotangent_low = gather_slots(cotangent.astype(BF16))

    query = product(normed_attn, full_attn[:, :part]).astype(BF16)
    key = product(normed_attn, full_attn[:, part : 2 * part]).astype(BF16)
    value = product(normed_attn, full_attn[:, 2 * part : 3 * part]).astype(BF16)
    gate_pre = product(normed_attn, full_attn[:, 3 * part : 4 * part])
    forget_pre = product(normed_attn, full_attn[:, 4 * part :])[:, :local_heads].astype(BF16)
    query = query.reshape(slots, local_heads, head_size)
    key = key.reshape(slots, local_heads, head_size)
    value = value.reshape(slots, local_heads, head_size)
    bias_local = lax.dynamic_slice_in_dim(forget_bias, rank * local_heads, local_heads)
    forget_total = forget_pre.astype(F32) + bias_local
    log_forget, pull_forget = jax.vjp(jax.nn.log_sigmoid, forget_total)
    cumulative = jnp.cumsum(log_forget, axis=0)
    head_output, log_totals = attention_forward(
        query, key, value, cumulative, length, scale, block
    )
    attended = head_output.reshape(slots, part).astype(F32)
    gated_full, pull_gate = jax.vjp(gate_product, attended, gate_pre)
    gated = gated_full.astype(BF16)
    middle = inputs + scatter_slots(product(gated, full_out))

    normed_ffn_full, pull_ffn_norm = jax.vjp(rms_norm, middle, norm_ffn)
    normed_ffn = gather_slots(normed_ffn_full.astype(BF16))
    gate_value = product(normed_ffn, full_gate_up[:, :local_units])
    up_value = product(normed_ffn, full_gate_up[:, local_units:])
    hidden_full, pull_swiglu = jax.vjp(swiglu, gate_value, up_value)
    hidden = hidden_full.astype(BF16)
    result = middle + scatter_slots(product(hidden, full_down))
    layer_output = result.astype(BF16)[None]

    grad_hidden = product_nt(cotangent_low, full_down)
    grad_gate_full, grad_up_full = pull_swiglu(grad_hidden)
    grad_gate_up = jnp.concatenate(
        [grad_gate_full.astype(BF16), grad_up_full.astype(BF16)], axis=1
    )
    grad_normed_ffn = scatter_slots(product_nt(grad_gate_up, full_gate_up))
    share_down = scatter_rows(product_tn(hidden, cotangent_low))
    share_gate_up = scatter_rows(product_tn(normed_ffn, grad_gate_up))
    grad_middle_part, grad_norm_ffn = pull_ffn_norm(grad_normed_ffn)
    grad_middle = cotangent + grad_middle_part
    grad_branch = gather_slots(grad_middle.astype(BF16))
    grad_gated = product_nt(grad_branch, full_out)
    grad_w_out = product_tn(gated, grad_branch).astype(BF16)
    share_out = scatter_rows(
        lax.all_to_all(grad_w_out, "seq", split_axis=1, concat_axis=0, tiled=True)
    )
    grad_attended_full, grad_gate_pre_full = pull_gate(grad_gated)
    grad_attended = grad_attended_full.astype(BF16).reshape(slots, local_heads, head_size)
    grad_gate_pre = grad_gate_pre_full.astype(BF16)
    grad_query, grad_key, grad_value, grad_cum = attention_backward(
        query, key, value, grad_attended, cumulative, log_totals, length, scale, block
    )
    grad_log_forget = jnp.flip(jnp.cumsum(jnp.flip(grad_cum, 0), axis=0), 0)
    grad_forget_total = pull_forget(grad_log_forget)[0]
    grad_bias_local = jnp.sum(grad_forget_total, axis=0)
    grad_bias = lax.dynamic_update_slice_in_dim(
        jnp.zeros((heads,), F32), grad_bias_local, rank * local_heads, 0
    )
    grad_attn = jnp.concatenate(
        [
            grad_query.reshape(slots, part),
            grad_key.reshape(slots, part),
            grad_value.reshape(slots, part),
            grad_gate_pre,
            jnp.pad(grad_forget_total.astype(BF16), ((0, 0), (0, pad))),
        ],
        axis=1,
    )
    grad_normed_attn = scatter_slots(product_nt(grad_attn, full_attn))
    share_attn = scatter_rows(product_tn(normed_attn, grad_attn))
    unused_normed, pull_attn_norm = jax.vjp(rms_norm, inputs, norm_attn)
    grad_input_part, grad_norm_attn = pull_attn_norm(grad_normed_attn)
    grad_input = (grad_middle + grad_input_part)[None]

    rows = w_query.shape[0]
    all_down = lax.all_gather(share_down, "seq", axis=0, tiled=True).astype(F32)
    all_gate_up = lax.all_gather(share_gate_up, "seq", axis=0, tiled=False)
    all_gate_up = all_gate_up.reshape(groups, rows, 2, owners, piece).transpose(2, 1, 3, 0, 4)
    all_gate_up = all_gate_up.reshape(2, rows, units).astype(F32)
    all_out = share_columns(share_out)
    all_attn = lax.all_gather(share_attn, "seq", axis=0, tiled=False)

    def whole(first, size):
        cut = all_attn[:, :, first : first + size].transpose(1, 0, 2)
        return cut.reshape(rows, groups * size).astype(F32)

    small = lax.psum((grad_norm_attn, grad_norm_ffn, grad_bias), ("seq", "wshard"))
    return (
        layer_output,
        grad_input,
        small[0],
        whole(0, part),
        whole(part, part),
        whole(2 * part, part),
        whole(3 * part, part),
        whole(4 * part, local_heads),
        small[2],
        all_out,
        small[1],
        all_gate_up[0],
        all_gate_up[1],
        all_down,
    )


def solution(mesh):
    rows = P("wshard", None)
    slots = P("wshard", "seq", None)
    return jax.shard_map(
        on_device,
        mesh=mesh,
        in_specs=(
            slots, P("wshard"), P(), rows, rows, rows, rows, rows, P(), rows, P(), rows, rows,
            rows, slots,
        ),
        out_specs=(
            slots, slots, P(), rows, rows, rows, rows, rows, P(), rows, P(), rows, rows, rows,
        ),
        check_vma=False,
    )
```

time: 2260 us -> 990 us (0.44)
  waiting for transfers between devices: 1780 us -> 623 us
  matrix products: 204 us -> 140 us
  blocking collectives: 131 us -> 73.6 us
  other arithmetic: 30 us -> 53.6 us
    reduce_scatter x8, waiting for transfers between devices: 1050 us -> 199 us  [the longest x4 104 us: scatter_rows(): lax.psum_scatter(partial.astype(BF16), 'wshard', scatter_dimension=0, til...]
    psum x1 -> x0, waiting for transfers between devices: 215 us -> none  [on_device(): lax.psum((share_query, share_key, share_value, share_ogate, share_forget,...]
    all_gather x8 -> x11, waiting for transfers between devices: 474 us -> 402 us  [the longest x4 171 us: gather_rows(): return lax.all_gather(shard, 'wshard', axis=0, tiled=True)]
    all_to_all x5 -> x1, blocking collectives: 58.3 us -> 18.7 us  [on_device(): lax.all_to_all(grad_w_out, 'seq', split_axis=1, concat_axis=0, tiled=True)]
    dot_general x8 -> x4, matrix products: 63.2 us -> 30.9 us  [product_tn(): lax.dot_general(left, right, (((0,), (0,)), ((), ())), preferred_element_...]
    unnamed x19, waiting for transfers between devices: 28.2 us -> 0.79 us
    dot_general x9 -> x4, matrix products: 47.6 us -> 33.1 us  [product_nt(): lax.dot_general(left, right, (((1,), (1,)), ((), ())), preferred_element_...]
  transfers between devices with their start and end apart: 23 -> 20, of which waited for: 18 -> 19; matrix products, arithmetic and copies ran while one was open for 11% -> 18% of each run, Pallas kernels for 0% -> 0%
where the time goes in v1:
time: 990 us; the launch traced here: 979 us
  waiting for transfers between devices  623 us (63%)
  matrix products  140 us (14%)
  blocking collectives  73.6 us (7%)
  local copies, waits for them, and re-layouts  68.3 us (7%)
  other arithmetic  53.6 us (5%)
  between operations  15.9 us (2%)
    all_gather x4, waiting for transfers between devices, gather_rows(): return lax.all_gather(shard, 'wshard', axis=0, tiled=True)  171 us
    all_gather x4, waiting for transfers between devices, gather_slots(): return lax.all_gather(shard, 'seq', axis=0, tiled=True)  135 us
    reduce_scatter x4, waiting for transfers between devices, scatter_rows(): lax.psum_scatter(partial.astype(BF16), 'wshard', scatter_dimension=0, til...  104 us
    reduce_scatter x4, waiting for transfers between devices, scatter_slots(): lax.psum_scatter(partial.astype(BF16), 'seq', scatter_dimension=0, tiled=...  95.2 us
    dot_general x9, matrix products, product(): return jnp.dot(left, right, preferred_element_type=F32)  44.1 us
    psum x1, blocking collectives, on_device(): lax.psum((grad_norm_attn, grad_norm_ffn, grad_bias), ('seq', 'wshard'))  40.3 us
    all_gather x1, waiting for transfers between devices, on_device(): all_attn = lax.all_gather(share_attn, 'seq', axis=0, tiled=False)  36.9 us
    dot_general x4, matrix products, product_nt(): lax.dot_general(left, right, (((1,), (1,)), ((), ())), preferred_element_...  33.1 us
  transfers between devices with their start and end apart: 20, of which 19 were waited for; matrix products, arithmetic and copies ran while one was open for 18% of the time, Pallas kernels for 0%

profile of v1, /device:TPU:0, one launch (start us, length us, event | category | flops | bytes accessed | tf_op | source)
XLA Modules:
  0.0 979.1 jit_solution(494081339802589565)
XLA Ops:
  19.4 16.4 %all-gather.18.cloned.1.call-done = bf16[1536,384]{1,0:T(8,128)(2,1)} async-done(((bf16[192,384]{1,0:T(8,128)(2,1)}), bf16[1536,384]{1,0:T(8,128)(2,1)}) %all-gather.18.cloned.1.call-update) | async-done | bytes 1179664 | tf_op jit(solution)/shard_map/all_gather | solution.py:37
  41.4 21.1 %all-to-all-done = bf16[4,384,384]{2,1,0:T(8,128)(2,1)S(1)} async-done(((bf16[4,384,384]{2,1,0:T(8,128)(2,1)}), bf16[4,384,384]{2,1,0:T(8,128)(2,1)S(1)}, u32[]{:S(2)}, u32[]{:S(2)}) %all-to-all-start) | async-done | bytes 1179680 | tf_op jit(solution)/shard_map/all_to_all | solution.py:170
  64.0 23.1 %all-gather.14.cloned.1.call-done = bf16[1024,1536]{1,0:T(8,128)(2,1)} async-done(((bf16[256,1536]{1,0:T(8,128)(2,1)}), bf16[1024,1536]{1,0:T(8,128)(2,1)}) %all-gather.14.cloned.1.call-update) | async-done | bytes 3145744 | tf_op jit(solution)/shard_map/all_gather | solution.py:45
  87.0 57.1 %all-gather.16.cloned.1.call-done = bf16[1536,1664]{1,0:T(8,128)(2,1)} async-done(((bf16[192,1664]{1,0:T(8,128)(2,1)}), bf16[1536,1664]{1,0:T(8,128)(2,1)}) %all-gather.16.cloned.1.call-update) | async-done | bytes 5111824 | tf_op jit(solution)/shard_map/all_gather | solution.py:37
  199.1 25.4 %reduce-scatter.9.cloned.1.call-done = bf16[256,1536]{1,0:T(8,128)(2,1)} async-done(((bf16[1024,1536]{1,0:T(8,128)(2,1)}), bf16[256,1536]{1,0:T(8,128)(2,1)}) %reduce-scatter.9.cloned.1.call-update) | async-done | bytes 786448 | tf_op jit(solution)/shard_map/reduce_scatter | solution.py:49
  228.6 42.1 %all-gather.26.cloned.1.call-done = bf16[1024,1536]{1,0:T(8,128)(2,1)} async-done(((bf16[256,1536]{1,0:T(8,128)(2,1)}), bf16[1024,1536]{1,0:T(8,128)(2,1)}) %all-gather.26.cloned.1.call-update) | async-done | bytes 3145744 | tf_op jit(solution)/shard_map/all_gather | solution.py:45
  270.7 40.3 %all-gather.24.cloned.1.call-done = bf16[1024,1536]{1,0:T(8,128)(2,1)} async-done(((bf16[128,1536]{1,0:T(8,128)(2,1)}), bf16[1024,1536]{1,0:T(8,128)(2,1)}) %all-gather.24.cloned.1.call-update) | async-done | bytes 3145744 | tf_op jit(solution)/shard_map/all_gather | solution.py:37
  319.2 57.6 %all-gather.22.cloned.1.call-done = bf16[1536,2048]{1,0:T(8,128)(2,1)} async-done(((bf16[192,2048]{1,0:T(8,128)(2,1)}), bf16[1536,2048]{1,0:T(8,128)(2,1)}) %all-gather.22.cloned.1.call-update) | async-done | bytes 6291472 | tf_op jit(solution)/shard_map/all_gather | solution.py:37
  376.8 44.9 %all-gather.20.cloned.1.call-done = bf16[1024,1536]{1,0:T(8,128)(2,1)} async-done(((bf16[256,1536]{1,0:T(8,128)(2,1)}), bf16[1024,1536]{1,0:T(8,128)(2,1)}) %all-gather.20.cloned.1.call-update) | async-done | bytes 3145744 | tf_op jit(solution)/shard_map/all_gather | solution.py:45
  440.1 9.4 convolution_convert_fusion.2
  449.8 43.8 %reduce-scatter.13.cloned.1.call-done = bf16[256,1536]{1,0:T(8,128)(2,1)} async-done(((bf16[1024,1536]{1,0:T(8,128)(2,1)}), bf16[256,1536]{1,0:T(8,128)(2,1)}) %reduce-scatter.13.cloned.1.call-update) | async-done | bytes 786448 | tf_op jit(solution)/shard_map/reduce_scatter | solution.py:49
  506.4 11.6 %convolution_convert_fusion.1 = bf16[1536,2048]{1,0:T(8,128)(2,1)} fusion(bf16[1024,1536]{1,0:T(8,128)(2,1)} %all-gather.20.cloned.1.call-done, bf16[1024,1024]{0,1:T(8,128)(2,1)} %get-tuple-element.150, bf16[1024,1024]{0,1:T(8,128)(2,1)} %copy-done.58), kind=kOutput, calls=%fused_computation.7 | convolution fusion | flops 6453985280 | bytes 13631488 | tf_op jit(solution)/shard_map/dot_general | solution.py:17
  518.2 24.6 %all-gather.28.cloned.1.call-done = bf16[1024,1536]{1,0:T(8,128)(2,1)} async-done(((bf16[256,1536]{1,0:T(8,128)(2,1)}), bf16[1024,1536]{1,0:T(8,128)(2,1)}) %all-gather.28.cloned.1.call-update) | async-done | bytes 3145744 | tf_op jit(solution)/shard_map/all_gather | solution.py:45
  607.5 18.7 %all_to_all.38 = bf16[384,4,384]{2,0,1:T(8,128)(2,1)} all-to-all(bf16[384,4,384]{2,0,1:T(8,128)(2,1)S(1)} %bitcast.215), channel_id=1, replica_groups=mesh['seq'=4,'wshard'=8] {'seq'}, dimensions={1} | all-to-all | bytes 2359296 | tf_op jit(solution)/shard_map/all_to_all | solution.py:220
  626.3 30.9 %reduce-scatter.21.cloned.1.call-done = bf16[192,2048]{1,0:T(8,128)(2,1)} async-done(((bf16[1536,2048]{1,0:T(8,128)(2,1)}), bf16[192,2048]{1,0:T(8,128)(2,1)}) %reduce-scatter.21.cloned.1.call-update) | async-done | bytes 786448 | tf_op jit(solution)/shard_map/reduce_scatter | solution.py:41
  657.3 10.2 %convolution_convert_fusion.3 = bf16[1024,1536]{1,0:T(8,128)(2,1)} fusion(bf16[1024,1664]{0,1:T(8,128)(2,1)} %copy-done.36, bf16[1536,1664]{1,0:T(8,128)(2,1)} %all-gather.16.cloned.1.call-done), kind=kOutput, calls=%fused_computation.25 | convolution fusion | flops 5236064256 | bytes 11665408 | tf_op jit(solution)/shard_map/dot_general | solution.py:21
  675.3 41.3 %reduce-scatter.17.cloned.1.call-done = bf16[192,1664]{1,0:T(8,128)(2,1)} async-done(((bf16[1536,1664]{1,0:T(8,128)(2,1)}), bf16[192,1664]{1,0:T(8,128)(2,1)}) %reduce-scatter.17.cloned.1.call-update) | async-done | bytes 638992 | tf_op jit(solution)/shard_map/reduce_scatter | solution.py:41
  716.7 31.0 %all-gather.30.cloned.1.call-done = bf16[512,1536]{1,0:T(8,128)(2,1)} async-done(((bf16[128,1536]{1,0:T(8,128)(2,1)}), bf16[512,1536]{1,0:T(8,128)(2,1)}) %all-gather.30.cloned.1.call-update) | async-done | bytes 1572880 | tf_op jit(solution)/shard_map/all_gather | solution.py:251
  751.3 31.5 %reduce-scatter.19.cloned.1.call-done = bf16[192,384]{1,0:T(8,128)(2,1)} async-done(((bf16[1536,384]{1,0:T(8,128)(2,1)}), bf16[192,384]{1,0:T(8,128)(2,1)}) %reduce-scatter.19.cloned.1.call-update) | async-done | bytes 147472 | tf_op jit(solution)/shard_map/reduce_scatter | solution.py:41
  782.8 14.5 %all_gather.52 = bf16[192,1536]{1,0:T(8,128)(2,1)S(1)} all-gather(bf16[192,384]{1,0:T(8,128)(2,1)} %reduce-scatter.19.cloned.1.call-done), channel_id=1, replica_groups=mesh['seq'=4,'wshard'=8] {'seq'}, dimensions={1}, use_global_device_ids=true | all-gather | bytes 737280 | tf_op jit(solution)/shard_map/all_gather | solution.py:55
  798.5 28.2 %all-gather.34.cloned.1.call-done = bf16[768,2048]{1,0:T(8,128)(2,1)} async-done(((bf16[192,2048]{1,0:T(8,128)(2,1)}), bf16[768,2048]{1,0:T(8,128)(2,1)}) %all-gather.34.cloned.1.call-update) | async-done | bytes 3145744 | tf_op jit(solution)/shard_map/all_gather | solution.py:252
  852.9 20.6 %reduce-scatter.15.cloned.1.call-done = bf16[256,1536]{1,0:T(8,128)(2,1)} async-done(((bf16[1024,1536]{1,0:T(8,128)(2,1)}), bf16[256,1536]{1,0:T(8,128)(2,1)}) %reduce-scatter.15.cloned.1.call-update) | async-done | bytes 786448 | tf_op jit(solution)/shard_map/reduce_scatter | solution.py:49
  875.4 40.3 %all-reduce.5 = (f32[1536]{0:T(1024)}, f32[24]{0:T(128)}, f32[1536]{0:T(1024)}) all-reduce(f32[1536]{0:T(1024)S(1)} %get-tuple-element.140, f32[24]{0:T(128)S(1)} %negate_dynamic-update-slice_fusion, f32[1536]{0:T(1024)S(1)} %copy-done.41), channel_id=1, replica_groups=mesh['seq'=4,'wshard'=8] {'seq','wshard'}, use_global_device_ids=true, to_apply=%region_23.24 | all-reduce | flops 3096 | bytes 24768 | tf_op jit(solution)/shard_map/psum | solution.py:262
  925.1 36.9 %all-gather.32.cloned.1.call-done = bf16[768,1664]{1,0:T(8,128)(2,1)} async-done(((bf16[192,1664]{1,0:T(8,128)(2,1)}), bf16[768,1664]{1,0:T(8,128)(2,1)}) %all-gather.32.cloned.1.call-update) | async-done | bytes 2555920 | tf_op jit(solution)/shard_map/all_gather | solution.py:256
  (305 shorter events, 241.4 us)
Async XLA Ops:
  7.2 176.8 %copy-start = (bf16[512,1536]{1,0:T(8,128)(2,1)S(1)}, bf16[512,1536]{1,0:T(8,128)(2,1)}, u32[]{:S(2)}) copy-start(bf16[512,1536]{1,0:T(8,128)(2,1)} %param.50) | copy-start | bytes 4718596
  7.2 28.6 %all-gather.18.cloned.1.call-start = ((), (), s32[]{:S(2)}) async-start(), calls=%async_computation.12 | async-start | bytes 1327104 | tf_op jit(solution)/shard_map/all_gather | solution.py:37
  9.0 78.1 %all-gather.14.cloned.1.call-start = ((), (), s32[]{:S(2)}) async-start(), calls=%async_computation.10 | async-start | bytes 3932160 | tf_op jit(solution)/shard_map/all_gather | solution.py:45
  13.8 130.4 %all-gather.16.cloned.1.call-start = ((), (), s32[]{:S(2)}) async-start(), calls=%async_computation.11 | async-start | bytes 5750784 | tf_op jit(solution)/shard_map/all_gather | solution.py:37
  35.8 26.8 %all-to-all-start = ((bf16[4,384,384]{2,1,0:T(8,128)(2,1)}), bf16[4,384,384]{2,1,0:T(8,128)(2,1)S(1)}, u32[]{:S(2)}, u32[]{:S(2)}) async-start(bf16[4,384,384]{2,1,0:T(8,128)(2,1)} %bitcast.248), calls=%async_computation | async-start | bytes 2359296 | tf_op jit(solution)/shard_map/all_to_all | solution.py:170
  39.3 185.2 %reduce-scatter.9.cloned.1.call-start = ((), (), s32[]{:S(2)}) async-start(), calls=%async_computation.13 | async-start | bytes 3932160 | tf_op jit(solution)/shard_map/reduce_scatter | solution.py:49
  40.1 107.2 %copy-start.52 = (f32[6]{0:T(128)}, f32[6]{0:T(128)S(1)}, u32[]{:S(2)}) copy-start(f32[6]{0:T(128)S(1)} %dynamic_slice.36) | copy-start | bytes 76
  181.7 89.0 %all-gather.26.cloned.1.call-start = ((), (), s32[]{:S(2)}) async-start(), calls=%async_computation.18 | async-start | bytes 3932160 | tf_op jit(solution)/shard_map/all_gather | solution.py:45
  182.8 313.2 %copy-start.46 = (f32[256]{0:T(256)}, f32[256]{0:T(256)S(1)}, u32[]{:S(2)}) copy-start(f32[256]{0:T(256)S(1)} %compare_convert_fusion) | copy-start | bytes 3076
  183.9 127.1 %all-gather.24.cloned.1.call-start = ((), (), s32[]{:S(2)}) async-start(), calls=%async_computation.16 | async-start | bytes 3538944 | tf_op jit(solution)/shard_map/all_gather | solution.py:37
  184.8 192.1 %all-gather.22.cloned.1.call-start = ((), (), s32[]{:S(2)}) async-start(), calls=%async_computation.15 | async-start | bytes 7077888 | tf_op jit(solution)/shard_map/all_gather | solution.py:37
  199.0 222.7 %all-gather.20.cloned.1.call-start = ((), (), s32[]{:S(2)}) async-start(), calls=%async_computation.14 | async-start | bytes 3932160 | tf_op jit(solution)/shard_map/all_gather | solution.py:45
  226.0 270.0 %copy-start.42 = (f32[256]{0:T(256)}, f32[256]{0:T(256)S(1)}, u32[]{:S(2)}) copy-start(f32[256]{0:T(256)S(1)} %fusion.73) | copy-start | bytes 3076
  228.3 265.2 %reduce-scatter.13.cloned.1.call-start = ((), (), s32[]{:S(2)}) async-start(), calls=%async_computation.19 | async-start | bytes 3932160 | tf_op jit(solution)/shard_map/reduce_scatter | solution.py:49
  449.5 93.2 %all-gather.28.cloned.1.call-start = ((), (), s32[]{:S(2)}) async-start(), calls=%async_computation.20 | async-start | bytes 3932160 | tf_op jit(solution)/shard_map/all_gather | solution.py:45
  498.7 104.3 %reduce-scatter.23.cloned.1.call-start = ((), (), s32[]{:S(2)}) async-start(), calls=%async_computation.25 | async-start | bytes 3538944 | tf_op jit(solution)/shard_map/reduce_scatter | solution.py:41
  506.4 150.9 %reduce-scatter.21.cloned.1.call-start = ((), (), s32[]{:S(2)}) async-start(), calls=%async_computation.24 | async-start | bytes 7077888 | tf_op jit(solution)/shard_map/reduce_scatter | solution.py:41
  518.1 198.6 %reduce-scatter.17.cloned.1.call-start = ((), (), s32[]{:S(2)}) async-start(), calls=%async_computation.22 | async-start | bytes 5750784 | tf_op jit(solution)/shard_map/reduce_scatter | solution.py:41
  603.0 144.8 %all-gather.30.cloned.1.call-start = ((), (), s32[]{:S(2)}) async-start(), calls=%async_computation.26 | async-start | bytes 1966080 | tf_op jit(solution)/shard_map/all_gather | solution.py:251
  603.5 179.3 %reduce-scatter.19.cloned.1.call-start = ((), (), s32[]{:S(2)}) async-start(), calls=%async_computation.23 | async-start | bytes 1327104 | tf_op jit(solution)/shard_map/reduce_scatter | solution.py:41
  626.3 200.5 %all-gather.34.cloned.1.call-start = ((), (), s32[]{:S(2)}) async-start(), calls=%async_computation.28 | async-start | bytes 3932160 | tf_op jit(solution)/shard_map/all_gather | solution.py:252
  657.3 216.2 %reduce-scatter.15.cloned.1.call-start = ((), (), s32[]{:S(2)}) async-start(), calls=%async_computation.21 | async-start | bytes 3932160 | tf_op jit(solution)/shard_map/reduce_scatter | solution.py:49
  667.5 253.6 %reduce-scatter.11.cloned.1.call-start = ((), (), s32[]{:S(2)}) async-start(), calls=%async_computation.17 | async-start | bytes 3932160 | tf_op jit(solution)/shard_map/reduce_scatter | solution.py:49
  675.3 286.6 %all-gather.32.cloned.1.call-start = ((), (), s32[]{:S(2)}) async-start(), calls=%async_computation.27 | async-start | bytes 3194880 | tf_op jit(solution)/shard_map/all_gather | solution.py:256
  (65 other events, 887.3 us)
Sparse Core Ops, SparseCore 0:
  10.2 25.4 all-gather.17
  38.2 48.8 all-gather.13
  89.3 54.8 all-gather.15
  181.8 42.6 reduce-scatter.8
  226.8 43.8 all-gather.25
  272.7 38.2 all-gather.23
  313.2 63.5 all-gather.21
  379.2 42.4 all-gather.19
  449.6 43.8 reduce-scatter.12
  498.8 43.8 all-gather.27
  545.6 40.3 reduce-scatter.22
  588.2 69.0 reduce-scatter.20
  659.6 57.0 reduce-scatter.16
  718.4 29.3 all-gather.29
  749.9 32.9 reduce-scatter.18
  784.5 42.1 all-gather.33
  829.6 43.8 reduce-scatter.14
  876.4 44.6 reduce-scatter.10
  922.9 38.9 all-gather.31
